TPU v7x, 32 devices: a whole 2x2x4 slice. The times are simulated.
32 devices in a mesh: groups: 2 (over y), seq: 8 (over z, x), vocab: 1, batch: 2 (over core).
Axes of the slice: x: 2, y: 2, z: 4, core: 2. Of those that a mesh axis runs over, the one named last changes fastest.
Arguments:
- queries: bfloat16 [4, 1536, 3584], P(('groups', 'vocab', 'batch'), 'seq'), parts along dimension 0, may hold values from -300 to 300
- keys: bfloat16 [4, 1536, 512], P(('groups', 'vocab', 'batch'), 'seq'), parts along dimension 0, may hold values from -10 to 10
- values: bfloat16 [4, 1536, 512], P(('groups', 'vocab', 'batch'), 'seq'), parts along dimension 0, may hold values from -24 to 24
- residual: bfloat16 [4, 1536, 3584], P(('groups', 'vocab', 'batch'), 'seq'), parts along dimension 0, may hold values from -2048 to 2048
- norm_gain: float32 [3584], replicated, may hold values from 0.5 to 1.5
Outputs:
- normed: bfloat16 [4, 1536, 3584], P(('groups', 'vocab', 'batch'), 'seq'), parts along dimension 0
There are 2 independent parts, one for each index of `groups`. A program takes and returns all parts, laid end to end along the dimension named above; an argument that names none is the same for every part. Nothing has to cross between parts.
All inputs are finite; a program needn't handle non-finite values.
Results may differ from a plain program's by a relative error of at most 0.0049.
Values may be sent and summed in bfloat16 or wider, within the bound.
A program may use at most 128 MiB of HBM per device.

v0:
```python
import math

import jax
import jax.numpy as jnp
from jax import lax
from jax.sharding import PartitionSpec as P

HEAD_WIDTH = 128


group_slots = 8
norm_eps = 1e-06


def attend_block(query_block, key_seen, value_seen, first_row):
    scores = jnp.einsum("qhd,kd->hqk", query_block, key_seen, preferred_element_type=jnp.float32)
    scores = scores * (1.0 / math.sqrt(query_block.shape[2]))
    query_pos = first_row + jnp.arange(query_block.shape[0])
    key_pos = jnp.arange(key_seen.shape[0])
    allowed = key_pos[None, :] <= query_pos[:, None]
    scores = jnp.where(allowed[None], scores, -jnp.inf)
    row_max = jnp.max(scores, axis=2, keepdims=True)
    weights = jnp.exp(scores - row_max)
    soft_probs = (weights / jnp.sum(weights, axis=2, keepdims=True)).astype(jnp.bfloat16)
    output = jnp.einsum("hqk,kd->qhd", soft_probs, value_seen, preferred_element_type=jnp.float32)
    return output.astype(jnp.bfloat16)


def body(queries, keys, values, residual, norm_gain):
    seq_count = lax.axis_size("seq")
    seq_rows = queries.shape[1]
    total_rows = seq_rows * seq_count
    kv_heads = keys.shape[2] // HEAD_WIDTH
    q_heads = queries.shape[2] // HEAD_WIDTH
    queries_per_group = q_heads // kv_heads
    padded = kv_heads * group_slots
    local_heads = padded // seq_count
    query_rows = queries[0].reshape(seq_rows, kv_heads, queries_per_group, HEAD_WIDTH)
    query_pad = jnp.pad(
        query_rows, ((0, 0), (0, 0), (0, group_slots - queries_per_group), (0, 0))
    ).reshape(seq_rows, padded * HEAD_WIDTH)
    key_rows = keys[0].reshape(seq_rows, kv_heads, HEAD_WIDTH)
    value_rows = values[0].reshape(seq_rows, kv_heads, HEAD_WIDTH)
    key_send = jnp.repeat(key_rows, seq_count // kv_heads, axis=1).reshape(
        seq_rows, seq_count * HEAD_WIDTH
    )
    value_send = jnp.repeat(value_rows, seq_count // kv_heads, axis=1).reshape(
        seq_rows, seq_count * HEAD_WIDTH
    )
    query_here, key_here, value_here = (
        lax.all_to_all(query_pad, "seq", split_axis=1, concat_axis=0, tiled=True),
        lax.all_to_all(key_send, "seq", split_axis=1, concat_axis=0, tiled=True),
        lax.all_to_all(value_send, "seq", split_axis=1, concat_axis=0, tiled=True),
    )
    query_here = query_here.reshape(total_rows, local_heads, HEAD_WIDTH)
    block_rows = 512
    outputs = []
    for block_index in range(total_rows // block_rows):
        first_row = block_index * block_rows
        last_row = first_row + block_rows
        outputs.append(
            attend_block(
                query_here[first_row:last_row],
                key_here[:last_row],
                value_here[:last_row],
                first_row,
            )
        )
    attended = jnp.concatenate(outputs, axis=0).reshape(total_rows, local_heads * HEAD_WIDTH)
    returned = lax.all_to_all(attended, "seq", split_axis=0, concat_axis=1, tiled=True)
    attention = returned.reshape(seq_rows, kv_heads, group_slots, HEAD_WIDTH)[
        :, :, :queries_per_group
    ].reshape(seq_rows, q_heads * HEAD_WIDTH)
    hidden = residual[0].astype(jnp.float32) + attention.astype(jnp.float32)
    inv_rms = lax.rsqrt(jnp.mean(hidden * hidden, axis=1, keepdims=True) + norm_eps)
    normed = (hidden * inv_rms * norm_gain).astype(jnp.bfloat16)
    return normed[None]


def solution(mesh):
    return jax.shard_map(
        body,
        mesh=mesh,
        in_specs=(
            P(("groups", "vocab", "batch"), "seq", None),
            P(("groups", "vocab", "batch"), "seq", None),
            P(("groups", "vocab", "batch"), "seq", None),
            P(("groups", "vocab", "batch"), "seq", None),
            P(),
        ),
        out_specs=P(("groups", "vocab", "batch"), "seq", None),
        check_vma=False,
    )
```

profile of v0, /device:TPU:0, one launch (start us, length us, event | category | flops | bytes accessed | tf_op | source)
XLA Modules:
  0.0 180.9 jit_solution(12698471071452616194)
XLA Ops:
  0.0 3.1 %reshape_squeeze.9 = bf16[192,4,7,128]{3,2,1,0:T(8,128)(2,1)S(1)} reshape(bf16[1,192,3584]{2,1,0:T(8,128)(2,1)} %param.5) | data formatting | bytes 2752512 | tf_op jit(solution)/shard_map/reshape;squeeze | solution.py:38
  3.4 1.0 all_to_all.52
  4.5 1.6 copy.17
  6.1 7.3 %all-to-all-start = ((bf16[192,8,512]{2,0,1:T(8,128)(2,1)}), bf16[192,8,512]{2,0,1:T(8,128)(2,1)S(1)}, u32[]{:S(2)}, u32[]{:S(2)}) async-start(bf16[192,8,512]{2,0,1:T(8,128)(2,1)} %copy.17), calls=%async_computation | async-start | bytes 3145728 | tf_op jit(solution)/shard_map/all_to_all | solution.py:51
  14.2 0.8 iota_compare_fusion.2
  15.1 1.2 iota_compare_fusion.1
  16.2 34.2 %all-to-all-done = bf16[192,8,512]{2,0,1:T(8,128)(2,1)S(1)} async-done(((bf16[192,8,512]{2,0,1:T(8,128)(2,1)}), bf16[192,8,512]{2,0,1:T(8,128)(2,1)S(1)}, u32[]{:S(2)}, u32[]{:S(2)}) %all-to-all-start) | async-done | bytes 1572896 | tf_op jit(solution)/shard_map/all_to_all | solution.py:51
  50.4 0.8 broadcast_in_dim.41
  51.2 3.6 %all-to-all-start.1 = ((bf16[192,8,128]{2,0,1:T(8,128)(2,1)}), bf16[192,8,128]{2,0,1:T(8,128)(2,1)S(1)}, u32[]{:S(2)}, u32[]{:S(2)}) async-start(bf16[192,8,128]{2,0,1:T(8,128)(2,1)} %bitcast.1), calls=%async_computation.1 | async-start | bytes 786432 | tf_op jit(solution)/shard_map/all_to_all | solution.py:52
  54.8 1.4 iota_compare_fusion
  57.2 9.5 %all-to-all-done.1 = bf16[192,8,128]{2,0,1:T(8,128)(2,1)S(1)} async-done(((bf16[192,8,128]{2,0,1:T(8,128)(2,1)}), bf16[192,8,128]{2,0,1:T(8,128)(2,1)S(1)}, u32[]{:S(2)}, u32[]{:S(2)}) %all-to-all-start.1) | async-done | bytes 393248 | tf_op jit(solution)/shard_map/all_to_all | solution.py:52
  66.7 1.8 broadcast_in_dim.43
  68.4 3.6 %all-to-all-start.2 = ((bf16[192,8,128]{2,0,1:T(8,128)(2,1)}), bf16[192,8,128]{2,0,1:T(8,128)(2,1)S(1)}, u32[]{:S(2)}, u32[]{:S(2)}) async-start(bf16[192,8,128]{2,0,1:T(8,128)(2,1)} %bitcast.6), calls=%async_computation.2 | async-start | bytes 786432 | tf_op jit(solution)/shard_map/all_to_all | solution.py:53
  72.1 0.7 fusion.43
  72.8 3.9 %fusion.65 = (f32[4,512]{1,0:T(4,128)S(1)}, f32[4,512,512]{1,2,0:T(8,128)}) fusion(f32[512,4,512]{0,2,1:T(8,128)S(1)} %fusion.43, pred[512,512]{0,1:T(8,128)(4,1)S(1)} %copy-done.4), kind=kOutput, calls=%fused_computation.76 | output fusion | flops 6291967 | bytes 8658944 | tf_op jit(solution)/shard_map/sub | solution.py:23
  76.7 5.3 %fusion.60 = (f32[4,512]{1,0:T(4,128)S(1)}, f32[4,512,1024]{2,1,0:T(8,128)}) fusion(pred[512,1024]{1,0:T(8,128)(4,1)S(1)} %copy-done.3, bf16[512,4,128]{2,1,0:T(4,128)(2,1)S(1)} %get-tuple-element.6, bf16[1536,128]{1,0:T(8,128)(2,1)S(1)} %bitcast.87), kind=kOutput, calls=%fused_computation.75 | convolution fusion | flops 545260544 | bytes 9707520 | tf_op jit(solution)/shard_map/sub | solution.py:23
  82.0 1.8 %all-to-all-done.2 = bf16[192,8,128]{2,0,1:T(8,128)(2,1)S(1)} async-done(((bf16[192,8,128]{2,0,1:T(8,128)(2,1)}), bf16[192,8,128]{2,0,1:T(8,128)(2,1)S(1)}, u32[]{:S(2)}, u32[]{:S(2)}) %all-to-all-start.2) | async-done | bytes 393248 | tf_op jit(solution)/shard_map/all_to_all | solution.py:53
  83.8 3.1 %fusion.38 = bf16[512,4,128]{2,0,1:T(8,128)(2,1)S(1)} fusion(f32[4,512,512]{1,2,0:T(8,128)} %get-tuple-element.13, f32[4,512]{1,0:T(4,128)S(1)} %get-tuple-element.12, bf16[1536,128]{1,0:T(8,128)(2,1)S(1)} %bitcast.89), kind=kOutput, calls=%fused_computation.50 | convolution fusion | flops 270794752 | bytes 4857856 | tf_op jit(solution)/shard_map/hqk,kd->qhd/dot_general | solution.py:25
  87.0 1.5 copy-done.8
  88.5 1.4 fusion.37
  89.9 6.4 %fusion.41 = f32[512,4,1536]{2,0,1:T(8,128)} fusion(bf16[1536,128,1]{1,0,2:T(8,128)(2,1)S(1)} %bitcast.88, bf16[512,4,128]{2,1,0:T(4,128)(2,1)S(1)} %get-tuple-element.7), kind=kOutput, calls=%fused_computation.53 | convolution fusion | flops 805306368 | bytes 13500416 | tf_op jit(solution)/shard_map/qhd,kd->hqk/dot_general | solution.py:16
  96.2 16.0 %fusion.59 = (f32[4,512]{1,0:T(4,128)S(1)}, f32[4,512,1536]{2,1,0:T(8,128)}) fusion(f32[512,4,1536]{2,0,1:T(8,128)} %fusion.41, pred[512,1536]{1,0:T(8,128)(4,1)S(1)} %copy-done.2), kind=kOutput, calls=%fused_computation.74 | output fusion | flops 18875904 | bytes 25960448 | tf_op jit(solution)/shard_map/sub | solution.py:23
  112.2 6.4 %fusion.36 = bf16[512,4,128]{2,0,1:T(8,128)(2,1)S(1)} fusion(bf16[1536,128,1]{1,0,2:T(8,128)(2,1)S(1)} %bitcast.91, f32[4,512,1536]{2,1,0:T(8,128)} %get-tuple-element.9, f32[4,512]{1,0:T(4,128)S(1)} %get-tuple-element.8), kind=kOutput, calls=%fused_computation.48 | convolution fusion | flops 811859968 | bytes 13508608 | tf_op jit(solution)/shard_map/hqk,kd->qhd/dot_general | solution.py:25
  118.7 7.3 %copy.24 = bf16[1536,4,128]{2,1,0:T(4,128)(2,1)S(1)} copy(bf16[1536,4,128]{2,0,1:T(8,128)(2,1)S(1)} %pad_maximum_fusion) | data formatting | bytes 3145728 | tf_op jit(solution)/shard_map/concatenate | solution.py:69
  126.7 40.6 %all_to_all.70 = bf16[8,192,512]{2,1,0:T(8,128)(2,1)S(1)} all-to-all(bf16[8,192,512]{2,1,0:T(8,128)(2,1)S(1)} %all_to_all.63), channel_id=1, replica_groups=mesh['groups'=2,'seq'=8,'vocab'=1,'batch'=2] {'seq'}, dimensions={0} | all-to-all | bytes 3145728 | tf_op jit(solution)/shard_map/all_to_all | solution.py:70
  167.3 0.9 copy.25
  168.2 2.3 %reshape.130 = bf16[192,4,8,128]{3,2,1,0:T(8,128)(2,1)} reshape(bf16[192,8,512]{2,1,0:T(8,128)(2,1)S(1)} %copy.25) | data formatting | bytes 3145728 | tf_op jit(solution)/shard_map/reshape | solution.py:71
  170.4 1.8 %slice_convert_fusion = f32[192,4,7,128]{3,2,1,0:T(8,128)S(1)} fusion(bf16[192,4,8,128]{3,2,1,0:T(8,128)(2,1)} %reshape.130), kind=kLoop, calls=%fused_computation.43 | loop fusion | flops 688128 | bytes 4128768 | tf_op jit(solution)/shard_map/convert_element_type | solution.py:74
  172.3 1.9 %reshape.133 = f32[192,3584]{1,0:T(8,128)} reshape(f32[192,4,7,128]{3,2,1,0:T(8,128)S(1)} %slice_convert_fusion) | data formatting | bytes 5505024 | tf_op jit(solution)/shard_map/convert_element_type | solution.py:74
  174.1 1.8 %reshape.131 = f32[1,192,3584]{2,1,0:T(8,128)} reshape(f32[192,4,7,128]{3,2,1,0:T(8,128)S(1)} %slice_convert_fusion) | data formatting | bytes 5505024 | tf_op jit(solution)/shard_map/convert_element_type | solution.py:74
  175.9 2.8 %fusion.28 = f32[192]{0:T(256)S(1)} fusion(f32[192,3584]{1,0:T(8,128)} %reshape.133, bf16[1,192,3584]{2,1,0:T(8,128)(2,1)} %param.8), kind=kLoop, calls=%fused_computation.37 | loop fusion | flops 2752320 | bytes 4129536 | tf_op jit(solution)/shard_map/reduce_sum | solution.py:75
  179.4 1.6 fusion.25
  (29 shorter events, 3.5 us)
Async XLA Ops:
  3.4 10.0 %copy-start.5 = (bf16[1,192,512]{2,1,0:T(8,128)(2,1)S(1)}, bf16[1,192,512]{2,1,0:T(8,128)(2,1)}, u32[]{:S(2)}) copy-start(bf16[1,192,512]{2,1,0:T(8,128)(2,1)} %param.6) | copy-start | bytes 589828
  4.4 9.0 %copy-start.6 = (bf16[1,192,512]{2,1,0:T(8,128)(2,1)S(1)}, bf16[1,192,512]{2,1,0:T(8,128)(2,1)}, u32[]{:S(2)}) copy-start(bf16[1,192,512]{2,1,0:T(8,128)(2,1)} %param.7) | copy-start | bytes 589828
  6.1 44.3 %all-to-all-start = ((bf16[192,8,512]{2,0,1:T(8,128)(2,1)}), bf16[192,8,512]{2,0,1:T(8,128)(2,1)S(1)}, u32[]{:S(2)}, u32[]{:S(2)}) async-start(bf16[192,8,512]{2,0,1:T(8,128)(2,1)} %copy.17), calls=%async_computation | async-start | bytes 3145728 | tf_op jit(solution)/shard_map/all_to_all | solution.py:51
  51.2 15.5 %all-to-all-start.1 = ((bf16[192,8,128]{2,0,1:T(8,128)(2,1)}), bf16[192,8,128]{2,0,1:T(8,128)(2,1)S(1)}, u32[]{:S(2)}, u32[]{:S(2)}) async-start(bf16[192,8,128]{2,0,1:T(8,128)(2,1)} %bitcast.1), calls=%async_computation.1 | async-start | bytes 786432 | tf_op jit(solution)/shard_map/all_to_all | solution.py:52
  57.2 15.6 %copy-start.4 = (pred[512,512]{0,1:T(8,128)(4,1)S(1)}, pred[512,512]{0,1:T(8,128)(4,1)}, u32[]{:S(2)}) copy-start(pred[512,512]{0,1:T(8,128)(4,1)} %iota_compare_fusion.2) | copy-start | bytes 786436
  68.4 15.4 %all-to-all-start.2 = ((bf16[192,8,128]{2,0,1:T(8,128)(2,1)}), bf16[192,8,128]{2,0,1:T(8,128)(2,1)S(1)}, u32[]{:S(2)}, u32[]{:S(2)}) async-start(bf16[192,8,128]{2,0,1:T(8,128)(2,1)} %bitcast.6), calls=%async_computation.2 | async-start | bytes 786432 | tf_op jit(solution)/shard_map/all_to_all | solution.py:53
  72.8 4.0 %copy-start.3 = (pred[512,1024]{1,0:T(8,128)(4,1)S(1)}, pred[512,1024]{1,0:T(8,128)(4,1)}, u32[]{:S(2)}) copy-start(pred[512,1024]{1,0:T(8,128)(4,1)} %iota_compare_fusion.1) | copy-start | bytes 1572868
  83.8 4.6 %copy-start.8 = (f32[4,512,1024]{2,1,0:T(8,128)S(1)}, f32[4,512,1024]{2,1,0:T(8,128)}, u32[]{:S(2)}) copy-start(f32[4,512,1024]{2,1,0:T(8,128)} %get-tuple-element.11) | copy-start | bytes 25165828
  89.8 6.4 %copy-start.2 = (pred[512,1536]{1,0:T(8,128)(4,1)S(1)}, pred[512,1536]{1,0:T(8,128)(4,1)}, u32[]{:S(2)}) copy-start(pred[512,1536]{1,0:T(8,128)(4,1)} %iota_compare_fusion) | copy-start | bytes 2359300
  174.1 4.6 %copy-start.7 = (f32[3584]{0:T(1024)S(1)}, f32[3584]{0:T(1024)}, u32[]{:S(2)}) copy-start(f32[3584]{0:T(1024)} %param.9) | copy-start | bytes 43012
  175.9 3.0 %copy-start = (f32[1,192,3584]{2,1,0:T(8,128)S(1)}, f32[1,192,3584]{2,1,0:T(8,128)}, u32[]{:S(2)}) copy-start(f32[1,192,3584]{2,1,0:T(8,128)} %reshape.131) | copy-start | bytes 8257540
  175.9 3.4 %copy-start.1 = (bf16[1,192,3584]{2,1,0:T(8,128)(2,1)S(1)}, bf16[1,192,3584]{2,1,0:T(8,128)(2,1)}, u32[]{:S(2)}) copy-start(bf16[1,192,3584]{2,1,0:T(8,128)(2,1)} %param.8) | copy-start | bytes 4128772
where the time goes:
time: 181 us
  waiting for transfers between devices  45.5 us (25%)
  blocking collectives  40.6 us (22%)
  other arithmetic  29.5 us (16%)
  local copies, waits for them, and re-layouts  27.3 us (15%)
  matrix products  23.2 us (13%)
  starting transfers between devices  14.6 us (8%)
    all_to_all x1, blocking collectives, body(): lax.all_to_all(attended, 'seq', split_axis=0, concat_axis=1, tiled=True)  40.6 us
    all_to_all x1, waiting for transfers between devices, body(): lax.all_to_all(query_pad, 'seq', split_axis=1, concat_axis=0, tiled=True)  34.2 us
    sub x2, other arithmetic, attend_block(): weights = jnp.exp(scores - row_max)  19.9 us
    dot_general x3, matrix products, attend_block(): jnp.einsum('hqk,kd->qhd', soft_probs, value_seen, preferred_element_type=...  10.9 us
    all_to_all x1, waiting for transfers between devices, body(): lax.all_to_all(key_send, 'seq', split_axis=1, concat_axis=0, tiled=True)  9.5 us
    concatenate x1, local copies, waits for them, and re-layouts, body(): jnp.concatenate(outputs, axis=0)  7.33 us
    all_to_all x1, starting transfers between devices, body(): lax.all_to_all(query_pad, 'seq', split_axis=1, concat_axis=0, tiled=True)  7.28 us
    dot_general x2, matrix products, attend_block(): jnp.einsum('qhd,kd->hqk', query_block, key_seen, preferred_element_type=j...  7.08 us
  transfers between devices with their start and end apart: 3, of which 3 were waited for; matrix products, arithmetic and copies ran while one was open for 8% of the time, Pallas kernels for 0%

commit v1 on v0

v1 whole, which is shorter than its diff:
```python
import functools
import math

import jax
import jax.numpy as jnp
from jax import lax
from jax.experimental import pallas as pl
from jax.experimental.pallas import tpu as pltpu
from jax.sharding import PartitionSpec as P

HEAD_WIDTH = 128
norm_eps = 1e-06
MESH = pl.DeviceIdType.MESH


def kernel(
    planes,
    rows,
    kv_heads,
    per_group,
    q_hbm,
    k_hbm,
    v_hbm,
    r_hbm,
    gain_ref,
    out_ref,
    qbuf,
    rbuf,
    kvbuf,
    top,
    acc,
    local_sem,
    up_send,
    up_recv,
    side_send,
    side_recv,
):
    W = HEAD_WIDTH
    width = kv_heads * per_group * W
    me = lax.axis_index("seq")
    plane = me // 2
    col = lax.rem(me, 2)
    above = me + 2
    below = me - 2
    side = me + 1 - 2 * col
    has_up = plane + 1 < planes
    has_down = plane > 0
    factor = math.log2(math.e) / math.sqrt(W)

    def own_copy(kind, src):
        return pltpu.make_async_copy(src.at[0], kvbuf.at[kind, me], local_sem.at[kind])

    own_k = own_copy(0, k_hbm)
    own_v = own_copy(1, v_hbm)
    q_in = pltpu.make_async_copy(q_hbm.at[0], qbuf, local_sem.at[2])
    r_in = pltpu.make_async_copy(r_hbm.at[0], rbuf, local_sem.at[3])
    own_k.start()
    own_v.start()
    q_in.start()
    r_in.start()

    barrier = pltpu.get_barrier_semaphore()
    pl.semaphore_signal(barrier, inc=1, device_id={"seq": side}, device_id_type=MESH)

    @pl.when(has_up)
    def _():
        pl.semaphore_signal(barrier, inc=1, device_id={"seq": above}, device_id_type=MESH)

    @pl.when(has_down)
    def _():
        pl.semaphore_signal(barrier, inc=1, device_id={"seq": below}, device_id_type=MESH)

    pl.semaphore_wait(barrier, 1 + has_up.astype(jnp.int32) + has_down.astype(jnp.int32))

    def up_copy(kind, q, column):
        slot = kvbuf.at[kind, 2 * q + column]
        return pltpu.make_async_remote_copy(
            src_ref=slot,
            dst_ref=slot,
            send_sem=up_send.at[kind, q],
            recv_sem=up_recv.at[kind, q],
            device_id={"seq": above},
            device_id_type=MESH,
        )

    def side_copy(kind, q, column):
        slot = kvbuf.at[kind, 2 * q + column]
        return pltpu.make_async_remote_copy(
            src_ref=slot,
            dst_ref=slot,
            send_sem=side_send.at[kind, q],
            recv_sem=side_recv.at[kind, q],
            device_id={"seq": side},
            device_id_type=MESH,
        )

    for kind, own in ((0, own_k), (1, own_v)):
        own.wait()

        @pl.when(has_up)
        def _(kind=kind):
            up_copy(kind, plane, col).start()

        @pl.when(col == 0)
        def _(kind=kind):
            side_copy(kind, plane, col).start()

    @pl.when(col == 0)
    def _():
        kvbuf[0, me + 1] = jnp.zeros((rows, kv_heads * W), jnp.bfloat16)
        kvbuf[1, me + 1] = jnp.zeros((rows, kv_heads * W), jnp.bfloat16)

    q_in.wait()

    def relay(q):
        for kind in (0, 1):
            up_copy(kind, q, col).wait_recv()

            @pl.when(has_up)
            def _(kind=kind):
                up_copy(kind, q, col).start()

            side_copy(kind, q, col).start()

    def attend(q, first):
        def one_group(g, carry):
            lanes = pl.ds(pl.multiple_of(g * W, W), W)
            keys = kvbuf[0, pl.ds(2 * q, 2), :, lanes].reshape(2 * rows, W)
            vals = kvbuf[1, pl.ds(2 * q, 2), :, lanes].reshape(2 * rows, W)
            vals = jnp.concatenate([vals, jnp.ones_like(vals)], axis=1)
            for j in range(per_group):
                head = g * per_group + j
                query = qbuf[:, pl.ds(pl.multiple_of(head * W, W), W)]
                s = lax.dot_general(
                    query, keys, (((1,), (1,)), ((), ())), preferred_element_type=jnp.float32
                )
                if first:
                    at_row = lax.broadcasted_iota(jnp.int32, s.shape, 0) + col * rows
                    at_key = lax.broadcasted_iota(jnp.int32, s.shape, 1)
                    s = jnp.where(at_key <= at_row, s, -jnp.inf)
                high = jnp.max(s, axis=1, keepdims=True)
                if not first:
                    old = top[head]
                    high = jnp.maximum(old[:, :1], high)
                w = jnp.exp2((s - high) * factor).astype(jnp.bfloat16)
                o = jnp.dot(w, vals, preferred_element_type=jnp.float32)
                wide = jnp.broadcast_to(high, (rows, W))
                if not first:
                    fade = jnp.exp2((old - wide) * factor)
                    o = o + acc[head] * jnp.concatenate([fade, fade], axis=1)
                top[head] = wide
                acc[head] = o
            return carry

        lax.fori_loop(0, kv_heads, one_group, 0)

    @pl.when(has_down)
    def _():
        relay(plane - 1)

    @pl.when(col == 1)
    def _():
        side_copy(0, plane, 1 - col).wait_recv()
        side_copy(1, plane, 1 - col).wait_recv()

    attend(plane, True)

    def step(t, carry):
        @pl.when(t <= plane)
        def _():
            relay(plane - t)

        q = plane - t + 1
        side_copy(0, q, 1 - col).wait_recv()
        side_copy(1, q, 1 - col).wait_recv()
        attend(q, False)
        return carry

    lax.fori_loop(2, plane + 2, step, 0)

    r_in.wait()
    total = jnp.zeros((rows, W), jnp.float32)
    for head in range(kv_heads * per_group):
        lanes = slice(head * W, (head + 1) * W)
        both = acc[head]
        attended = (both[:, :W] / both[:, W:]).astype(jnp.bfloat16).astype(jnp.float32)
        hidden = rbuf[:, lanes].astype(jnp.float32) + attended
        total = total + hidden * hidden
        top[head] = hidden
    mean = jnp.sum(total, axis=1, keepdims=True) / width
    scale = jnp.broadcast_to(lax.rsqrt(mean + norm_eps), (rows, W))
    for head in range(kv_heads * per_group):
        lanes = slice(head * W, (head + 1) * W)
        out_ref[0, :, lanes] = (top[head] * scale * gain_ref[:, lanes]).astype(jnp.bfloat16)

    for kind in (0, 1):

        @pl.when(has_up)
        def _(kind=kind):
            up_copy(kind, plane, col).wait_send()

        @pl.when(col == 0)
        def _(kind=kind):
            side_copy(kind, plane, col).wait_send()

    def drain(q, carry):
        for kind in (0, 1):

            @pl.when(has_up)
            def _(kind=kind):
                up_copy(kind, q, col).wait_send()

            side_copy(kind, q, col).wait_send()
        return carry

    lax.fori_loop(0, plane, drain, 0)


def body(queries, keys, values, residual, norm_gain):
    count = lax.axis_size("seq")
    rows = queries.shape[1]
    width = queries.shape[2]
    kv_heads = keys.shape[2] // HEAD_WIDTH
    heads = width // HEAD_WIDTH
    planes = count // 2
    hbm = pl.BlockSpec(memory_space=pl.ANY)
    vmem = pl.BlockSpec(memory_space=pltpu.VMEM)
    return pl.pallas_call(
        functools.partial(kernel, planes, rows, kv_heads, heads // kv_heads),
        out_shape=jax.ShapeDtypeStruct(queries.shape, jnp.bfloat16),
        in_specs=[hbm, hbm, hbm, hbm, vmem],
        out_specs=vmem,
        scratch_shapes=[
            pltpu.VMEM((rows, width), jnp.bfloat16),
            pltpu.VMEM((rows, width), jnp.bfloat16),
            pltpu.VMEM((2, count, rows, keys.shape[2]), jnp.bfloat16),
            pltpu.VMEM((heads, rows, HEAD_WIDTH), jnp.float32),
            pltpu.VMEM((heads, rows, 2 * HEAD_WIDTH), jnp.float32),
            pltpu.SemaphoreType.DMA((4,)),
            pltpu.SemaphoreType.DMA((2, planes)),
            pltpu.SemaphoreType.DMA((2, planes)),
            pltpu.SemaphoreType.DMA((2, planes)),
            pltpu.SemaphoreType.DMA((2, planes)),
        ],
        compiler_params=pltpu.CompilerParams(
            collective_id=0, has_side_effects=True, vmem_limit_bytes=48 * 1024 * 1024
        ),
    )(queries, keys, values, residual, norm_gain.reshape(1, width))


def solution(mesh):
    rows = P(("groups", "vocab", "batch"), "seq", None)
    return jax.shard_map(
        body,
        mesh=mesh,
        in_specs=(rows, rows, rows, rows, P()),
        out_specs=rows,
        check_vma=False,
    )
```

time: 181 us -> 53.9 us (0.30)
  the two profiles are of different devices: /device:TPU:0 before, /device:TPU:30 now
where the time goes in v1:
time: 53.9 us; the launch traced here: 53 us
  Pallas kernels  46.6 us (86%)
  local copies, waits for them, and re-layouts  6.33 us (12%)
    pallas_call x1, Pallas kernels, body(): pl.pallas_call(functools.partial(kernel, planes, rows, kv_heads, heads //...  46.6 us
    unnamed x9, local copies, waits for them, and re-layouts  5.61 us

profile of v1, /device:TPU:30, one launch (start us, length us, event | category | flops | bytes accessed | tf_op | source)
XLA Modules:
  0.0 53.0 jit_solution(12822957878769025971)
XLA Ops:
  0.0 0.7 %reshape.3.gain_ref = f32[1,3584]{1,0:T(1,128)S(1)} reshape(f32[3584]{0:T(1024)} %param.9) | data formatting | bytes 28672 | tf_op jit(solution)/shard_map/reshape | solution.py:248
  0.7 0.0 copy-start
  0.7 1.3 %copy-done = bf16[1,192,3584]{2,1,0:T(8,128)(2,1)S(1)} copy-done((bf16[1,192,3584]{2,1,0:T(8,128)(2,1)S(1)}, bf16[1,192,3584]{2,1,0:T(8,128)(2,1)}, u32[]{:S(2)}) %copy-start) | copy-done | bytes 1376280
  2.1 0.0 copy-start.1
  2.1 1.3 %copy-done.1 = bf16[1,192,3584]{2,1,0:T(8,128)(2,1)S(1)} copy-done((bf16[1,192,3584]{2,1,0:T(8,128)(2,1)S(1)}, bf16[1,192,3584]{2,1,0:T(8,128)(2,1)}, u32[]{:S(2)}) %copy-start.1) | copy-done | bytes 1376280
  3.4 0.0 copy-start.2
  3.4 0.9 %copy-done.2 = bf16[1,192,512]{2,1,0:T(8,128)(2,1)S(1)} copy-done((bf16[1,192,512]{2,1,0:T(8,128)(2,1)S(1)}, bf16[1,192,512]{2,1,0:T(8,128)(2,1)}, u32[]{:S(2)}) %copy-start.2) | copy-done | bytes 196632
  4.3 0.0 copy-start.3
  4.3 0.9 %copy-done.3 = bf16[1,192,512]{2,1,0:T(8,128)(2,1)S(1)} copy-done((bf16[1,192,512]{2,1,0:T(8,128)(2,1)S(1)}, bf16[1,192,512]{2,1,0:T(8,128)(2,1)}, u32[]{:S(2)}) %copy-start.3) | copy-done | bytes 196632
  5.3 46.6 %shard_map.55 = bf16[1,192,3584]{2,1,0:T(8,128)(2,1)S(1)} custom-call(bf16[1,192,3584]{2,1,0:T(8,128)(2,1)S(1)} %copy-done, bf16[1,192,512]{2,1,0:T(8,128)(2,1)S(1)} %copy-done.2, bf16[1,192,512]{2,1,0:T(8,128)(2,1)S(1)} %copy-done.3, bf16[1,192,3584]{2,1,0:T(8,128)(2,1)S(1)} %copy-done.1, f32[1,3584]{1,0:T(1,128)S(1)} %reshape.3.gain_ref), custom_call_target="tpu_custom_call" | custom-call | tf_op jit(solution)/shard_map/pallas_call | solution.py:228
  51.9 1.1 %copy.7 = bf16[1,192,3584]{2,1,0:T(8,128)(2,1)} copy(bf16[1,192,3584]{2,1,0:T(8,128)(2,1)S(1)} %shard_map.55) | data formatting | bytes 2752512
Async XLA Ops:
  0.7 1.3 %copy-start = (bf16[1,192,3584]{2,1,0:T(8,128)(2,1)S(1)}, bf16[1,192,3584]{2,1,0:T(8,128)(2,1)}, u32[]{:S(2)}) copy-start(bf16[1,192,3584]{2,1,0:T(8,128)(2,1)} %q_hbm.1) | copy-start | bytes 4128772
  2.1 1.3 %copy-start.1 = (bf16[1,192,3584]{2,1,0:T(8,128)(2,1)S(1)}, bf16[1,192,3584]{2,1,0:T(8,128)(2,1)}, u32[]{:S(2)}) copy-start(bf16[1,192,3584]{2,1,0:T(8,128)(2,1)} %r_hbm.1) | copy-start | bytes 4128772
  3.4 0.9 %copy-start.2 = (bf16[1,192,512]{2,1,0:T(8,128)(2,1)S(1)}, bf16[1,192,512]{2,1,0:T(8,128)(2,1)}, u32[]{:S(2)}) copy-start(bf16[1,192,512]{2,1,0:T(8,128)(2,1)} %k_hbm.1) | copy-start | bytes 589828
  4.3 0.9 %copy-start.3 = (bf16[1,192,512]{2,1,0:T(8,128)(2,1)S(1)}, bf16[1,192,512]{2,1,0:T(8,128)(2,1)}, u32[]{:S(2)}) copy-start(bf16[1,192,512]{2,1,0:T(8,128)(2,1)} %v_hbm.1) | copy-start | bytes 589828

commit v2 on v1

v2 whole, which is shorter than its diff:
```python
import functools
import math

import jax
import jax.numpy as jnp
from jax import lax
from jax.experimental import pallas as pl
from jax.experimental.pallas import tpu as pltpu
from jax.sharding import PartitionSpec as P

HEAD_WIDTH = 128
norm_eps = 1e-06
MESH = pl.DeviceIdType.MESH


def kernel(
    planes,
    rows,
    kv_heads,
    per_group,
    q_hbm,
    k_hbm,
    v_hbm,
    r_hbm,
    gain_ref,
    out_ref,
    qbuf,
    rbuf,
    kvbuf,
    top,
    acc,
    squares,
    local_sem,
    own_sem,
    up_send,
    up_recv,
    side_send,
    side_recv,
    extra_send,
    extra_recv,
):
    W = HEAD_WIDTH
    width = kv_heads * per_group * W
    half = kv_heads // 2
    me = lax.axis_index("seq")
    plane = me // 2
    col = lax.rem(me, 2)
    above = me + 2
    below = me - 2
    side = me + 1 - 2 * col
    has_up = plane + 1 < planes
    has_down = plane > 0
    factor = math.log2(math.e) / math.sqrt(W)

    own = []
    for g in range(kv_heads):
        for kind, src in ((0, k_hbm), (1, v_hbm)):
            copy = pltpu.make_async_copy(
                src.at[0, :, pl.ds(g * W, W)],
                kvbuf.at[g, me, :, pl.ds(kind * W, W)],
                own_sem.at[g, kind],
            )
            copy.start()
            own.append(copy)
    q_in = pltpu.make_async_copy(q_hbm.at[0], qbuf, local_sem.at[0])
    r_in = pltpu.make_async_copy(r_hbm.at[0], rbuf, local_sem.at[1])
    q_in.start()
    r_in.start()

    barrier = pltpu.get_barrier_semaphore()
    pl.semaphore_signal(barrier, inc=1, device_id={"seq": side}, device_id_type=MESH)

    @pl.when(has_up)
    def _():
        pl.semaphore_signal(barrier, inc=1, device_id={"seq": above}, device_id_type=MESH)

    @pl.when(has_down)
    def _():
        pl.semaphore_signal(barrier, inc=1, device_id={"seq": below}, device_id_type=MESH)

    pl.semaphore_wait(barrier, 1 + has_up.astype(jnp.int32) + has_down.astype(jnp.int32))

    def remote(slot, send_sem, recv_sem, target):
        return pltpu.make_async_remote_copy(
            src_ref=slot,
            dst_ref=slot,
            send_sem=send_sem,
            recv_sem=recv_sem,
            device_id={"seq": target},
            device_id_type=MESH,
        )

    def up_copy(g, q):
        return remote(kvbuf.at[g, 2 * q + col], up_send.at[g, q], up_recv.at[g, q], above)

    def side_copy(g, q, column):
        return remote(kvbuf.at[g, 2 * q + column], side_send.at[g, q], side_recv.at[g, q], side)

    def extra_copy(g, q):
        return remote(kvbuf.at[g, 2 * q], extra_send.at[g], extra_recv.at[g], above)

    def by_extra(g, q, column):
        return (column == 1) & (q == plane - 1) & (g >= half)

    for g in range(kv_heads):
        own[2 * g].wait()
        own[2 * g + 1].wait()

        @pl.when(has_up)
        def _(g=g):
            up_copy(g, plane).start()

        @pl.when(col == 0)
        def _(g=g):
            side_copy(g, plane, col).start()

    @pl.when(col == 0)
    def _():
        for g in range(kv_heads):
            kvbuf[g, me + 1] = jnp.zeros((rows, 2 * W), jnp.bfloat16)

    squares[...] = jnp.zeros_like(squares)
    q_in.wait()
    r_in.wait()

    def relay(g, q):
        up_copy(g, q).wait_recv()

        @pl.when(has_up)
        def _():
            up_copy(g, q).start()

        @pl.when(jnp.logical_not(by_extra(g, q, 1 - col)))
        def _():
            side_copy(g, q, col).start()

    def attend(g, q, first):
        keys = kvbuf[g, pl.ds(2 * q, 2), :, :W].reshape(2 * rows, W)
        vals = kvbuf[g, pl.ds(2 * q, 2), :, W:].reshape(2 * rows, W)
        vals = jnp.concatenate([vals, jnp.ones_like(vals)], axis=1)
        for j in range(per_group):
            head = g * per_group + j
            query = qbuf[:, pl.ds(pl.multiple_of(head * W, W), W)]
            s = lax.dot_general(
                query, keys, (((1,), (1,)), ((), ())), preferred_element_type=jnp.float32
            )
            if first:
                at_row = lax.broadcasted_iota(jnp.int32, s.shape, 0) + col * rows
                at_key = lax.broadcasted_iota(jnp.int32, s.shape, 1)
                s = jnp.where(at_key <= at_row, s, -jnp.inf)
            high = jnp.max(s, axis=1, keepdims=True)
            if not first:
                old = top[head]
                high = jnp.maximum(old[:, :1], high)
            w = jnp.exp2((s - high) * factor).astype(jnp.bfloat16)
            o = jnp.dot(w, vals, preferred_element_type=jnp.float32)
            wide = jnp.broadcast_to(high, (rows, W))
            if not first:
                fade = jnp.exp2((old - wide) * factor)
                o = o + acc[head] * jnp.concatenate([fade, fade], axis=1)
            top[head] = wide
            acc[head] = o

    def finish(g):
        total = squares[...]
        for j in range(per_group):
            head = g * per_group + j
            lanes = pl.ds(pl.multiple_of(head * W, W), W)
            both = acc[head]
            attended = (both[:, :W] / both[:, W:]).astype(jnp.bfloat16).astype(jnp.float32)
            hidden = rbuf[:, lanes].astype(jnp.float32) + attended
            total = total + hidden * hidden
            top[head] = hidden
        squares[...] = total

    def diagonal(g, carry):
        @pl.when(has_down)
        def _():
            relay(g, plane - 1)

        @pl.when(col == 1)
        def _():
            side_copy(g, plane, 1 - col).wait_recv()

        @pl.when((col == 1) & has_up & (g >= half))
        def _():
            extra_copy(g, plane).start()

        attend(g, plane, True)

        @pl.when(plane == 0)
        def _():
            finish(g)

        return carry

    lax.fori_loop(0, kv_heads, diagonal, 0)

    def step(t, carry):
        q = plane - t + 1

        def one(g, inner):
            @pl.when(t <= plane)
            def _():
                relay(g, q - 1)

            @pl.when(by_extra(g, q, col))
            def _():
                extra_copy(g, q).wait_recv()

            @pl.when(jnp.logical_not(by_extra(g, q, col)))
            def _():
                side_copy(g, q, 1 - col).wait_recv()

            attend(g, q, False)

            @pl.when(q == 0)
            def _():
                finish(g)

            return inner

        return lax.fori_loop(0, kv_heads, one, carry)

    lax.fori_loop(2, plane + 2, step, 0)

    mean = jnp.sum(squares[...], axis=1, keepdims=True) / width
    scale = jnp.broadcast_to(lax.rsqrt(mean + norm_eps), (rows, W))
    for head in range(kv_heads * per_group):
        lanes = slice(head * W, (head + 1) * W)
        gain = gain_ref[lanes].reshape(1, W)
        out_ref[0, :, lanes] = (top[head] * scale * gain).astype(jnp.bfloat16)

    def drain_own(g, carry):
        @pl.when(has_up)
        def _():
            up_copy(g, plane).wait_send()

        @pl.when(col == 0)
        def _():
            side_copy(g, plane, col).wait_send()

        @pl.when((col == 1) & has_up & (g >= half))
        def _():
            extra_copy(g, plane).wait_send()

        return carry

    lax.fori_loop(0, kv_heads, drain_own, 0)

    def drain(q, carry):
        def one(g, inner):
            @pl.when(has_up)
            def _():
                up_copy(g, q).wait_send()

            @pl.when(jnp.logical_not(by_extra(g, q, 1 - col)))
            def _():
                side_copy(g, q, col).wait_send()

            return inner

        return lax.fori_loop(0, kv_heads, one, carry)

    lax.fori_loop(0, plane, drain, 0)


def body(queries, keys, values, residual, norm_gain):
    count = lax.axis_size("seq")
    rows = queries.shape[1]
    width = queries.shape[2]
    kv_heads = keys.shape[2] // HEAD_WIDTH
    heads = width // HEAD_WIDTH
    planes = count // 2
    hbm = pl.BlockSpec(memory_space=pltpu.HBM)
    vmem = pl.BlockSpec(memory_space=pltpu.VMEM)
    return pl.pallas_call(
        functools.partial(kernel, planes, rows, kv_heads, heads // kv_heads),
        out_shape=jax.ShapeDtypeStruct(queries.shape, jnp.bfloat16),
        in_specs=[hbm, hbm, hbm, hbm, vmem],
        out_specs=vmem,
        scratch_shapes=[
            pltpu.VMEM((rows, width), jnp.bfloat16),
            pltpu.VMEM((rows, width), jnp.bfloat16),
            pltpu.VMEM((kv_heads, count, rows, 2 * HEAD_WIDTH), jnp.bfloat16),
            pltpu.VMEM((heads, rows, HEAD_WIDTH), jnp.float32),
            pltpu.VMEM((heads, rows, 2 * HEAD_WIDTH), jnp.float32),
            pltpu.VMEM((rows, HEAD_WIDTH), jnp.float32),
            pltpu.SemaphoreType.DMA((2,)),
            pltpu.SemaphoreType.DMA((kv_heads, 2)),
            pltpu.SemaphoreType.DMA((kv_heads, planes)),
            pltpu.SemaphoreType.DMA((kv_heads, planes)),
            pltpu.SemaphoreType.DMA((kv_heads, planes)),
            pltpu.SemaphoreType.DMA((kv_heads, planes)),
            pltpu.SemaphoreType.DMA((kv_heads,)),
            pltpu.SemaphoreType.DMA((kv_heads,)),
        ],
        compiler_params=pltpu.CompilerParams(
            collective_id=0, has_side_effects=True, vmem_limit_bytes=48 * 1024 * 1024
        ),
    )(queries, keys, values, residual, norm_gain)


def solution(mesh):
    rows = P(("groups", "vocab", "batch"), "seq", None)
    return jax.shard_map(
        body,
        mesh=mesh,
        in_specs=(rows, rows, rows, rows, P()),
        out_specs=rows,
        check_vma=False,
    )
```

time: 53.9 us -> 52 us (0.965); the launches traced: 53 us -> 51.7 us
  Pallas kernels: 46.6 us -> 45.4 us
    pallas_call x1, Pallas kernels: 46.6 us -> 45.4 us  [body(): pl.pallas_call(functools.partial(kernel, planes, rows, kv_heads, heads //...]
    reshape x1 -> x0, local copies, waits for them, and re-layouts: 0.73 us -> none  [body(): norm_gain.reshape(1, width)]
    unnamed x9 -> x11, local copies, waits for them, and re-layouts: 5.61 us -> 6.33 us
where the time goes in v2:
time: 52 us; the launch traced here: 51.7 us
  Pallas kernels  45.4 us (87%)
  local copies, waits for them, and re-layouts  6.33 us (12%)
    pallas_call x1, Pallas kernels, body(): pl.pallas_call(functools.partial(kernel, planes, rows, kv_heads, heads //...  45.4 us
    unnamed x11, local copies, waits for them, and re-layouts  6.33 us

profile of v2, /device:TPU:30, one launch (start us, length us, event | category | flops | bytes accessed | tf_op | source)
XLA Modules:
  0.0 51.7 jit_solution(6405499948172073955)
XLA Ops:
  0.0 0.0 copy-start
  0.0 1.3 %copy-done = bf16[1,192,3584]{2,1,0:T(8,128)(2,1)S(1)} copy-done((bf16[1,192,3584]{2,1,0:T(8,128)(2,1)S(1)}, bf16[1,192,3584]{2,1,0:T(8,128)(2,1)}, u32[]{:S(2)}) %copy-start) | copy-done | bytes 1376280
  1.3 0.0 copy-start.1
  1.3 1.3 %copy-done.1 = bf16[1,192,3584]{2,1,0:T(8,128)(2,1)S(1)} copy-done((bf16[1,192,3584]{2,1,0:T(8,128)(2,1)S(1)}, bf16[1,192,3584]{2,1,0:T(8,128)(2,1)}, u32[]{:S(2)}) %copy-start.1) | copy-done | bytes 1376280
  2.7 0.0 copy-start.2
  2.7 0.9 %copy-done.2 = bf16[1,192,512]{2,1,0:T(8,128)(2,1)S(1)} copy-done((bf16[1,192,512]{2,1,0:T(8,128)(2,1)S(1)}, bf16[1,192,512]{2,1,0:T(8,128)(2,1)}, u32[]{:S(2)}) %copy-start.2) | copy-done | bytes 196632
  3.6 0.0 copy-start.3
  3.6 0.9 %copy-done.3 = bf16[1,192,512]{2,1,0:T(8,128)(2,1)S(1)} copy-done((bf16[1,192,512]{2,1,0:T(8,128)(2,1)S(1)}, bf16[1,192,512]{2,1,0:T(8,128)(2,1)}, u32[]{:S(2)}) %copy-start.3) | copy-done | bytes 196632
  4.5 0.0 copy-start.4
  4.5 0.7 %copy-done.4 = f32[3584]{0:T(1024)S(1)} copy-done((f32[3584]{0:T(1024)S(1)}, f32[3584]{0:T(1024)}, u32[]{:S(2)}) %copy-start.4) | copy-done | bytes 14360
  5.3 45.4 %shard_map.55 = bf16[1,192,3584]{2,1,0:T(8,128)(2,1)S(1)} custom-call(bf16[1,192,3584]{2,1,0:T(8,128)(2,1)S(1)} %copy-done, bf16[1,192,512]{2,1,0:T(8,128)(2,1)S(1)} %copy-done.2, bf16[1,192,512]{2,1,0:T(8,128)(2,1)S(1)} %copy-done.3, bf16[1,192,3584]{2,1,0:T(8,128)(2,1)S(1)} %copy-done.1, f32[3584]{0:T(1024)S(1)} %copy-done.4), custom_call_target="tpu_custom_call" | custom-call | tf_op jit(solution)/shard_map/pallas_call | solution.py:277
  50.7 1.1 %copy.7 = bf16[1,192,3584]{2,1,0:T(8,128)(2,1)} copy(bf16[1,192,3584]{2,1,0:T(8,128)(2,1)S(1)} %shard_map.55) | data formatting | bytes 2752512
Async XLA Ops:
  0.0 1.3 %copy-start = (bf16[1,192,3584]{2,1,0:T(8,128)(2,1)S(1)}, bf16[1,192,3584]{2,1,0:T(8,128)(2,1)}, u32[]{:S(2)}) copy-start(bf16[1,192,3584]{2,1,0:T(8,128)(2,1)} %q_hbm.1) | copy-start | bytes 4128772
  1.3 1.3 %copy-start.1 = (bf16[1,192,3584]{2,1,0:T(8,128)(2,1)S(1)}, bf16[1,192,3584]{2,1,0:T(8,128)(2,1)}, u32[]{:S(2)}) copy-start(bf16[1,192,3584]{2,1,0:T(8,128)(2,1)} %r_hbm.1) | copy-start | bytes 4128772
  2.7 0.9 %copy-start.2 = (bf16[1,192,512]{2,1,0:T(8,128)(2,1)S(1)}, bf16[1,192,512]{2,1,0:T(8,128)(2,1)}, u32[]{:S(2)}) copy-start(bf16[1,192,512]{2,1,0:T(8,128)(2,1)} %k_hbm.1) | copy-start | bytes 589828
  3.6 0.9 %copy-start.3 = (bf16[1,192,512]{2,1,0:T(8,128)(2,1)S(1)}, bf16[1,192,512]{2,1,0:T(8,128)(2,1)}, u32[]{:S(2)}) copy-start(bf16[1,192,512]{2,1,0:T(8,128)(2,1)} %v_hbm.1) | copy-start | bytes 589828
  4.5 0.7 %copy-start.4 = (f32[3584]{0:T(1024)S(1)}, f32[3584]{0:T(1024)}, u32[]{:S(2)}) copy-start(f32[3584]{0:T(1024)} %gain_ref.1) | copy-start | bytes 43012

commit v3 on v2

--- a/solution.py
+++ b/solution.py
@@ -41,7 +41,6 @@
 ):
     W = HEAD_WIDTH
     width = kv_heads * per_group * W
-    half = kv_heads // 2
     me = lax.axis_index("seq")
     plane = me // 2
     col = lax.rem(me, 2)
@@ -62,9 +61,16 @@
             )
             copy.start()
             own.append(copy)
-    q_in = pltpu.make_async_copy(q_hbm.at[0], qbuf, local_sem.at[0])
-    r_in = pltpu.make_async_copy(r_hbm.at[0], rbuf, local_sem.at[1])
-    q_in.start()
+    heads = kv_heads * per_group
+
+    def query_copy(head):
+        lanes = pl.ds(pl.multiple_of(head * W, W), W)
+        return pltpu.make_async_copy(
+            q_hbm.at[0, :, lanes], qbuf.at[head], local_sem.at[head]
+        )
+
+    lax.fori_loop(0, heads, lambda head, carry: query_copy(head).start(), None)
+    r_in = pltpu.make_async_copy(r_hbm.at[0], rbuf, local_sem.at[heads])
     r_in.start()
 
     barrier = pltpu.get_barrier_semaphore()
@@ -96,11 +102,11 @@
     def side_copy(g, q, column):
         return remote(kvbuf.at[g, 2 * q + column], side_send.at[g, q], side_recv.at[g, q], side)
 
-    def extra_copy(g, q):
-        return remote(kvbuf.at[g, 2 * q], extra_send.at[g], extra_recv.at[g], above)
+    def extra_copy(g):
+        return remote(kvbuf.at[g, 0], extra_send.at[g], extra_recv.at[g], above)
 
     def by_extra(g, q, column):
-        return (column == 1) & (q == plane - 1) & (g >= half)
+        return (column == 1) & (q == 0) & has_down & (lax.rem(g, 2) == 1)
 
     for g in range(kv_heads):
         own[2 * g].wait()
@@ -120,7 +126,7 @@
             kvbuf[g, me + 1] = jnp.zeros((rows, 2 * W), jnp.bfloat16)
 
     squares[...] = jnp.zeros_like(squares)
-    q_in.wait()
+    lax.fori_loop(0, heads, lambda head, carry: query_copy(head).wait(), None)
     r_in.wait()
 
     def relay(g, q):
@@ -138,23 +144,32 @@
         keys = kvbuf[g, pl.ds(2 * q, 2), :, :W].reshape(2 * rows, W)
         vals = kvbuf[g, pl.ds(2 * q, 2), :, W:].reshape(2 * rows, W)
         vals = jnp.concatenate([vals, jnp.ones_like(vals)], axis=1)
+
+        def scores(j):
+            return lax.dot_general(
+                qbuf[g * per_group + j],
+                keys,
+                (((1,), (1,)), ((), ())),
+                preferred_element_type=jnp.float32,
+            )
+
+        s_next = scores(0)
         for j in range(per_group):
             head = g * per_group + j
-            query = qbuf[:, pl.ds(pl.multiple_of(head * W, W), W)]
-            s = lax.dot_general(
-                query, keys, (((1,), (1,)), ((), ())), preferred_element_type=jnp.float32
-            )
+            s = s_next
+            if j + 1 < per_group:
+                s_next = scores(j + 1)
             if first:
                 at_row = lax.broadcasted_iota(jnp.int32, s.shape, 0) + col * rows
                 at_key = lax.broadcasted_iota(jnp.int32, s.shape, 1)
                 s = jnp.where(at_key <= at_row, s, -jnp.inf)
-            high = jnp.max(s, axis=1, keepdims=True)
+            wide = jnp.broadcast_to(jnp.max(s, axis=1, keepdims=True), (rows, W))
             if not first:
                 old = top[head]
-                high = jnp.maximum(old[:, :1], high)
-            w = jnp.exp2((s - high) * factor).astype(jnp.bfloat16)
+                wide = jnp.maximum(old, wide)
+            s = (s - jnp.concatenate([wide] * (2 * rows // W), axis=1)) * factor
+            w = jnp.exp2(s).astype(jnp.bfloat16)
             o = jnp.dot(w, vals, preferred_element_type=jnp.float32)
-            wide = jnp.broadcast_to(high, (rows, W))
             if not first:
                 fade = jnp.exp2((old - wide) * factor)
                 o = o + acc[head] * jnp.concatenate([fade, fade], axis=1)
@@ -182,9 +197,9 @@
         def _():
             side_copy(g, plane, 1 - col).wait_recv()
 
-        @pl.when((col == 1) & has_up & (g >= half))
-        def _():
-            extra_copy(g, plane).start()
+        @pl.when((col == 1) & (plane == 0) & has_up & (lax.rem(g, 2) == 1))
+        def _():
+            extra_copy(g).start()
 
         attend(g, plane, True)
 
@@ -206,7 +221,11 @@
 
             @pl.when(by_extra(g, q, col))
             def _():
-                extra_copy(g, q).wait_recv()
+                extra_copy(g).wait_recv()
+
+            @pl.when(by_extra(g, q, col) & has_up)
+            def _():
+                extra_copy(g).start()
 
             @pl.when(jnp.logical_not(by_extra(g, q, col)))
             def _():
@@ -240,9 +259,9 @@
         def _():
             side_copy(g, plane, col).wait_send()
 
-        @pl.when((col == 1) & has_up & (g >= half))
-        def _():
-            extra_copy(g, plane).wait_send()
+        @pl.when((col == 1) & has_up & (lax.rem(g, 2) == 1))
+        def _():
+            extra_copy(g).wait_send()
 
         return carry
 
@@ -280,13 +299,13 @@
         in_specs=[hbm, hbm, hbm, hbm, vmem],
         out_specs=vmem,
         scratch_shapes=[
-            pltpu.VMEM((rows, width), jnp.bfloat16),
+            pltpu.VMEM((heads, rows, HEAD_WIDTH), jnp.bfloat16),
             pltpu.VMEM((rows, width), jnp.bfloat16),
             pltpu.VMEM((kv_heads, count, rows, 2 * HEAD_WIDTH), jnp.bfloat16),
             pltpu.VMEM((heads, rows, HEAD_WIDTH), jnp.float32),
             pltpu.VMEM((heads, rows, 2 * HEAD_WIDTH), jnp.float32),
             pltpu.VMEM((rows, HEAD_WIDTH), jnp.float32),
-            pltpu.SemaphoreType.DMA((2,)),
+            pltpu.SemaphoreType.DMA((heads + 1,)),
             pltpu.SemaphoreType.DMA((kv_heads, 2)),
             pltpu.SemaphoreType.DMA((kv_heads, planes)),
             pltpu.SemaphoreType.DMA((kv_heads, planes)),
@@ -296,7 +315,7 @@
             pltpu.SemaphoreType.DMA((kv_heads,)),
         ],
         compiler_params=pltpu.CompilerParams(
-            collective_id=0, has_side_effects=True, vmem_limit_bytes=48 * 1024 * 1024
+            collective_id=0, has_side_effects=True, vmem_limit_bytes=67043328
         ),
     )(queries, keys, values, residual, norm_gain)
 

time: 52 us -> 43.2 us (0.83)
  Pallas kernels: 45.4 us -> 40.5 us
  local copies, waits for them, and re-layouts: 6.33 us -> 2.51 us
    pallas_call x1, Pallas kernels: 45.4 us -> 40.5 us  [body(): pl.pallas_call(functools.partial(kernel, planes, rows, kv_heads, heads //...]
    unnamed x11 -> x1, local copies, waits for them, and re-layouts: 6.33 us -> 2.51 us
where the time goes in v3:
time: 43.2 us; the launch traced here: 43 us
  Pallas kernels  40.5 us (94%)
  local copies, waits for them, and re-layouts  2.51 us (6%)
    pallas_call x1, Pallas kernels, body(): pl.pallas_call(functools.partial(kernel, planes, rows, kv_heads, heads //...  40.5 us
    unnamed x1, local copies, waits for them, and re-layouts  2.51 us

profile of v3, /device:TPU:30, one launch (start us, length us, event | category | flops | bytes accessed | tf_op | source)
XLA Modules:
  0.0 43.0 jit_solution(16476796082702185669)
XLA Ops:
  0.0 40.5 %shard_map.55 = bf16[1,192,3584]{2,1,0:T(8,128)(2,1)} custom-call(bf16[1,192,3584]{2,1,0:T(8,128)(2,1)} %q_hbm.1, bf16[1,192,512]{2,1,0:T(8,128)(2,1)} %k_hbm.1, bf16[1,192,512]{2,1,0:T(8,128)(2,1)} %v_hbm.1, bf16[1,192,3584]{2,1,0:T(8,128)(2,1)} %r_hbm.1, f32[3584]{0:T(1024)} %gain_ref.1), custom_call_target="tpu_custom_call" | custom-call | tf_op jit(solution)/shard_map/pallas_call | solution.py:296
  40.5 2.5 %copy.7 = bf16[1,192,3584]{2,1,0:T(8,128)(2,1)} copy(bf16[1,192,3584]{2,1,0:T(8,128)(2,1)} %shard_map.55) | data formatting | bytes 2752512

commit v4 on v3

--- a/solution.py
+++ b/solution.py
@@ -19,8 +19,7 @@
     kv_heads,
     per_group,
     q_hbm,
-    k_hbm,
-    v_hbm,
+    kv_hbm,
     r_hbm,
     gain_ref,
     out_ref,
@@ -53,14 +52,9 @@
 
     own = []
     for g in range(kv_heads):
-        for kind, src in ((0, k_hbm), (1, v_hbm)):
-            copy = pltpu.make_async_copy(
-                src.at[0, :, pl.ds(g * W, W)],
-                kvbuf.at[g, me, :, pl.ds(kind * W, W)],
-                own_sem.at[g, kind],
-            )
-            copy.start()
-            own.append(copy)
+        copy = pltpu.make_async_copy(kv_hbm.at[g], kvbuf.at[g, me], own_sem.at[g])
+        copy.start()
+        own.append(copy)
     heads = kv_heads * per_group
 
     def query_copy(head):
@@ -69,9 +63,7 @@
             q_hbm.at[0, :, lanes], qbuf.at[head], local_sem.at[head]
         )
 
-    lax.fori_loop(0, heads, lambda head, carry: query_copy(head).start(), None)
     r_in = pltpu.make_async_copy(r_hbm.at[0], rbuf, local_sem.at[heads])
-    r_in.start()
 
     barrier = pltpu.get_barrier_semaphore()
     pl.semaphore_signal(barrier, inc=1, device_id={"seq": side}, device_id_type=MESH)
@@ -109,8 +101,7 @@
         return (column == 1) & (q == 0) & has_down & (lax.rem(g, 2) == 1)
 
     for g in range(kv_heads):
-        own[2 * g].wait()
-        own[2 * g + 1].wait()
+        own[g].wait()
 
         @pl.when(has_up)
         def _(g=g):
@@ -119,6 +110,9 @@
         @pl.when(col == 0)
         def _(g=g):
             side_copy(g, plane, col).start()
+
+    lax.fori_loop(0, heads, lambda head, carry: query_copy(head).start(), None)
+    r_in.start()
 
     @pl.when(col == 0)
     def _():
@@ -291,12 +285,18 @@
     kv_heads = keys.shape[2] // HEAD_WIDTH
     heads = width // HEAD_WIDTH
     planes = count // 2
+    pairs = jnp.stack(
+        [
+            jnp.concatenate([x[0, :, g * HEAD_WIDTH : (g + 1) * HEAD_WIDTH] for x in (keys, values)], axis=1)
+            for g in range(kv_heads)
+        ]
+    )
     hbm = pl.BlockSpec(memory_space=pltpu.HBM)
     vmem = pl.BlockSpec(memory_space=pltpu.VMEM)
     return pl.pallas_call(
         functools.partial(kernel, planes, rows, kv_heads, heads // kv_heads),
         out_shape=jax.ShapeDtypeStruct(queries.shape, jnp.bfloat16),
-        in_specs=[hbm, hbm, hbm, hbm, vmem],
+        in_specs=[hbm, hbm, hbm, vmem],
         out_specs=vmem,
         scratch_shapes=[
             pltpu.VMEM((heads, rows, HEAD_WIDTH), jnp.bfloat16),
@@ -306,7 +306,7 @@
             pltpu.VMEM((heads, rows, 2 * HEAD_WIDTH), jnp.float32),
             pltpu.VMEM((rows, HEAD_WIDTH), jnp.float32),
             pltpu.SemaphoreType.DMA((heads + 1,)),
-            pltpu.SemaphoreType.DMA((kv_heads, 2)),
+            pltpu.SemaphoreType.DMA((kv_heads,)),
             pltpu.SemaphoreType.DMA((kv_heads, planes)),
             pltpu.SemaphoreType.DMA((kv_heads, planes)),
             pltpu.SemaphoreType.DMA((kv_heads, planes)),
@@ -315,9 +315,9 @@
             pltpu.SemaphoreType.DMA((kv_heads,)),
         ],
         compiler_params=pltpu.CompilerParams(
-            collective_id=0, has_side_effects=True, vmem_limit_bytes=67043328
+            collective_id=0, has_side_effects=True, vmem_limit_bytes=54500000
         ),
-    )(queries, keys, values, residual, norm_gain)
+    )(queries, pairs, residual, norm_gain)
 
 
 def solution(mesh):

time: 43.2 us -> 42.3 us (0.979)
  Pallas kernels: 40.5 us -> 39 us
    squeeze x0 -> x2, local copies, waits for them, and re-layouts: none -> 1.79 us  [body(): x[0, :, g * HEAD_WIDTH:(g + 1) * HEAD_WIDTH]]
    pallas_call x1, Pallas kernels: 40.5 us -> 39 us  [body(): pl.pallas_call(functools.partial(kernel, planes, rows, kv_heads, heads //...]
    unnamed x1 -> x3, local copies, waits for them, and re-layouts: 2.51 us -> 1.08 us
where the time goes in v4:
time: 42.3 us; the launch traced here: 42 us
  Pallas kernels  39 us (92%)
  local copies, waits for them, and re-layouts  2.88 us (7%)
    pallas_call x1, Pallas kernels, body(): pl.pallas_call(functools.partial(kernel, planes, rows, kv_heads, heads //...  39 us
    squeeze x2, local copies, waits for them, and re-layouts, body(): x[0, :, g * HEAD_WIDTH:(g + 1) * HEAD_WIDTH]  1.79 us
    unnamed x3, local copies, waits for them, and re-layouts  1.08 us

profile of v4, /device:TPU:30, one launch (start us, length us, event | category | flops | bytes accessed | tf_op | source)
XLA Modules:
  0.0 42.0 jit_solution(12914597102797522768)
XLA Ops:
  0.0 0.0 copy-start
  0.0 0.9 %slice_bitcast_fusion.7 = (bf16[192,128]{1,0:T(8,128)(2,1)S(1)}, bf16[192,128]{1,0:T(8,128)(2,1)S(1)}, bf16[192,128]{1,0:T(8,128)(2,1)S(1)}, bf16[192,128]{1,0:T(8,128)(2,1)S(1)}) fusion(bf16[1,192,512]{2,1,0:T(8,128)(2,1)} %param.6), kind=kLoop, calls=%fused_computation.12 | loop fusion | bytes 393216 | tf_op jit(solution)/shard_map/squeeze | solution.py:290
  0.9 0.9 %slice_bitcast_fusion.6 = (bf16[192,128]{1,0:T(8,128)(2,1)S(1)}, bf16[192,128]{1,0:T(8,128)(2,1)S(1)}, bf16[192,128]{1,0:T(8,128)(2,1)S(1)}, bf16[192,128]{1,0:T(8,128)(2,1)S(1)}) fusion(bf16[1,192,512]{2,1,0:T(8,128)(2,1)} %param.7), kind=kLoop, calls=%fused_computation.11 | loop fusion | bytes 393216 | tf_op jit(solution)/shard_map/squeeze | solution.py:290
  1.9 0.1 pad_maximum_fusion.kv_hbm
  1.9 0.0 copy-done
  1.9 39.0 %shard_map.55 = bf16[1,192,3584]{2,1,0:T(8,128)(2,1)S(1)} custom-call(bf16[1,192,3584]{2,1,0:T(8,128)(2,1)} %q_hbm.1, bf16[4,192,256]{2,1,0:T(8,128)(2,1)S(1)} %pad_maximum_fusion.kv_hbm, bf16[1,192,3584]{2,1,0:T(8,128)(2,1)} %r_hbm.1, f32[3584]{0:T(1024)S(1)} %copy-done), custom_call_target="tpu_custom_call" | custom-call | tf_op jit(solution)/shard_map/pallas_call | solution.py:296
  40.9 1.1 %copy.7 = bf16[1,192,3584]{2,1,0:T(8,128)(2,1)} copy(bf16[1,192,3584]{2,1,0:T(8,128)(2,1)S(1)} %shard_map.55) | data formatting | bytes 2752512
  (2 shorter events, 0.1 us)
Async XLA Ops:
  0.0 1.9 %copy-start = (f32[3584]{0:T(1024)S(1)}, f32[3584]{0:T(1024)}, u32[]{:S(2)}) copy-start(f32[3584]{0:T(1024)} %gain_ref.1) | copy-start | bytes 43012
